TPU v7x, 32 devices: a whole 2x2x4 slice. The times are simulated.
32 devices in a mesh: dom: 16 (over z, y, x), mp: 2 (over core).
Axes of the slice: x: 2, y: 2, z: 4, core: 2. Of those that a mesh axis runs over, the one named last changes fastest.
Arguments:
- table: bfloat16 [65536, 768], P('dom', 'mp'), may hold values from -6 to 6
- weight_a: bfloat16 [1536, 512], P(None, 'mp'), may hold values from -0.15625 to 0.15625
- bias_a: float32 [512], replicated, may hold values from -3 to 3
- weight_b: bfloat16 [1024, 512], P(None, 'mp'), may hold values from -0.25 to 0.25
- bias_b: float32 [512], replicated, may hold values from -3 to 3
- requests: int32 [16, 16, 128], P('dom'), may hold values from 0 to 4095
- near_a: int32 [16384, 10], P('dom'), may hold values from 0 to 2047
- self_a: int32 [16384], P('dom'), may hold values from 0 to 2047
- count_a: int32 [16384], P('dom'), may hold values from 1 to 10
- near_b: int32 [4096, 5], P('dom'), may hold values from 0 to 1023
- self_b: int32 [4096], P('dom'), may hold values from 0 to 1023
- count_b: int32 [4096], P('dom'), may hold values from 1 to 5
Outputs:
- embedding: bfloat16 [4096, 512], P('dom', 'mp')
Inputs may be any that keep to these rules, and one draw needn't show every extreme that they name: `requests`: local row indices at the owner. `near_a`: slots of the same minibatch; entries at j >= count_a are padding. `near_b`: positions within the same minibatch; entries at j >= count_b are padding.
All inputs are finite; a program needn't handle non-finite values.
Results may differ from a plain program's by a relative error of at most 0.0074.
Values may be sent and summed in bfloat16 or wider, within the bound.
A program may use at most 64 MiB of HBM per device.

v0:
```python
import jax
import jax.numpy as jnp
from jax import lax
from jax.sharding import PartitionSpec as P

F = 768
H = 512


def mean_rows(source, neighbours, counts):
    total_rows = neighbours.shape[0]
    fanout = neighbours.shape[1]
    block = min(512, total_rows)
    columns = lax.broadcasted_iota(jnp.int32, (1, source.shape[0]), 1)

    def one_block(pieces):
        near, valid = pieces
        weights = jnp.zeros((block, source.shape[0]), jnp.bfloat16)
        for column in range(fanout):
            picked = (near[:, column : column + 1] == columns) & (valid[:, None] > column)
            weights = weights + picked.astype(jnp.bfloat16)
        total = jnp.dot(weights, source, preferred_element_type=jnp.float32)
        return (total / valid[:, None].astype(jnp.float32)).astype(jnp.bfloat16)

    result = lax.map(one_block, (neighbours.reshape(-1, block, fanout), counts.reshape(-1, block)))
    return result.reshape(total_rows, source.shape[1])


def shards(
    table,
    weight_a,
    bias_a,
    weight_b,
    bias_b,
    requests,
    near_a,
    self_a,
    count_a,
    near_b,
    self_b,
    count_b,
):
    half_hidden = weight_a.shape[1]
    half_feature = table.shape[1]
    mp_index = lax.axis_index("mp")
    asked = requests[0]
    found = table[lax.all_to_all(asked, "dom", split_axis=0, concat_axis=0, tiled=True)]
    fetched = lax.all_to_all(found, "dom", split_axis=0, concat_axis=0, tiled=True)
    fetched = fetched.reshape(-1, half_feature)
    own_rows = fetched[self_a]
    mean_a = mean_rows(fetched, near_a, count_a)
    whole_a = lax.all_gather(weight_a, "mp", axis=1, tiled=True)
    own_weight = lax.dynamic_slice_in_dim(whole_a, mp_index * half_feature, half_feature, 0)
    near_weight = lax.dynamic_slice_in_dim(whole_a, F + mp_index * half_feature, half_feature, 0)
    partial_value = jnp.dot(own_rows, own_weight, preferred_element_type=jnp.float32)
    partial_value = partial_value + jnp.dot(mean_a, near_weight, preferred_element_type=jnp.float32)
    bias_part = lax.dynamic_slice_in_dim(bias_a, mp_index * half_hidden, half_hidden, 0)
    before = lax.psum_scatter(partial_value, "mp", scatter_dimension=1, tiled=True) + bias_part
    hidden_a = jax.nn.relu(before).astype(jnp.bfloat16)
    bias_part = lax.dynamic_slice_in_dim(bias_b, mp_index * half_hidden, half_hidden, 0)
    mean_b = mean_rows(hidden_a, near_b, count_b)
    own_b = lax.all_gather(hidden_a[self_b], "mp", axis=1, tiled=True)
    mean_whole = lax.all_gather(mean_b, "mp", axis=1, tiled=True)
    inputs_b = jnp.concatenate([own_b, mean_whole], axis=1)
    state = jax.nn.relu(jnp.dot(inputs_b, weight_b, preferred_element_type=jnp.float32) + bias_part)
    squares = lax.psum(jnp.sum(state * state, axis=1), "mp")
    scaled = state * jnp.sqrt(jnp.float32(H)) / jnp.sqrt(squares[:, None] + H)
    return scaled.astype(jnp.bfloat16)


def solution(mesh):
    placed = (
        P("dom", "mp"),
        P(None, "mp"),
        P(),
        P(None, "mp"),
        P(),
        P("dom", None, None),
        P("dom", None),
        P("dom"),
        P("dom"),
        P("dom", None),
        P("dom"),
        P("dom"),
    )
    return jax.shard_map(
        shards, mesh=mesh, in_specs=placed, out_specs=P("dom", "mp"), check_vma=False
    )
```

profile of v0, /device:TPU:0, one launch (start us, length us, event | category | flops | bytes accessed | tf_op | source)
XLA Modules:
  0.0 135.9 jit_solution(11270580848167446451)
XLA Ops:
  6.5 0.0 copy-start
  6.5 15.8 %all_to_all.17 = s32[16,1,128]{2,1,0:T(1,128)S(1)} all-to-all(s32[16,1,128]{2,1,0:T(1,128)} %bitcast.82), channel_id=1, replica_groups=mesh['dom'=16,'mp'=2] {'dom'}, dimensions={0} | all-to-all | bytes 16384 | tf_op jit(solution)/shard_map/all_to_all | solution.py:47
  22.4 0.0 copy-done
  22.4 9.0 %gather_fusion = bf16[2048,384]{1,0:T(8,128)(2,1)} fusion(bf16[4096,384]{1,0:T(8,128)(2,1)S(1)} %copy-done, s32[2048]{0:T(1024)S(1)} %fusion.112), kind=kCustom, calls=%fused_computation | custom fusion | bytes 3153920 | tf_op jit(solution)/shard_map/gather | solution.py:47
  31.4 0.0 copy-start.4
  31.4 0.0 copy-start.2
  31.4 0.0 copy-start.5
  31.4 4.5 %all-to-all-start.1 = ((bf16[16,128,384]{2,1,0:T(8,128)(2,1)}), bf16[16,128,384]{2,1,0:T(8,128)(2,1)}, u32[]{:S(2)}, u32[]{:S(2)}) async-start(bf16[16,128,384]{2,1,0:T(8,128)(2,1)} %bitcast.67), calls=%async_computation.1 | async-start | bytes 3145728 | tf_op jit(solution)/shard_map/all_to_all | solution.py:48
  36.0 0.0 all-gather.3.cloned.1.call-start
  36.0 0.7 all-gather.3.cloned.1.call-update
  36.7 0.0 reduce-scatter.2.cloned.1.call-start
  36.8 0.0 copy-done.4
  36.8 0.0 copy-done.2
  36.8 0.0 copy-done.5
  36.9 32.3 %all-to-all-done.1 = bf16[16,128,384]{2,1,0:T(8,128)(2,1)} async-done(((bf16[16,128,384]{2,1,0:T(8,128)(2,1)}), bf16[16,128,384]{2,1,0:T(8,128)(2,1)}, u32[]{:S(2)}, u32[]{:S(2)}) %all-to-all-start.1) | async-done | bytes 1572896 | tf_op jit(solution)/shard_map/all_to_all | solution.py:48
  69.2 22.4 %while.16 = (s32[]{:T(128)}, bf16[2,512,384]{2,1,0:T(8,128)(2,1)}, s32[2,512,10]{1,0,2:T(2,128)S(1)}, s32[2,512]{1,0:T(2,128)S(1)}, bf16[2048,384]{1,0:T(8,128)(2,1)}, /*index=5*/s32[]{:T(128)}) while((s32[]{:T(128)}, bf16[2,512,384]{2,1,0:T(8,128)(2,1)}, s32[2,512,10]{1,0,2:T(2,128)S(1)}, s32[2,512]{1,0:T(2,128)S(1)}, ...), condition=%wide.region_1.2_spmd.clone.clone, body=%wide.region_0.1_spmd.clone.clone.sunk | while | flops 858134016 | bytes 2130009 | solution.py:25
  69.2 0.1 compare_reduce_fusion.11
  69.3 11.0 %fusion.134 = bf16[2,512,384]{2,1,0:T(8,128)(2,1)} fusion(bf16[2,512,384]{2,1,0:T(8,128)(2,1)} %get-tuple-element.255, s32[]{:T(128)S(6)} %copy.27, bf16[2048,384]{1,0:T(8,128)(2,1)} %get-tuple-element.264, s32[512]{0:T(512)S(1)} %bitcast.71, s32[512]{0:T(512)S(1)} %bitcast.72, s32[512]{0:T(512)S(1)} %bitcast.73, s32[512]{0:T(512)S(1)} %bitcast.74, ...), kind=kOutput, calls=%fused_computation.67.clone.1 | convolution fusion | flops 858128384 | bytes 1993732 | tf_op jit(solution)/shard_map/while/body/eval_jaxpr/dot_general | solution.py:22
  80.4 0.1 compare_reduce_fusion.11
  80.5 11.0 %fusion.134 = bf16[2,512,384]{2,1,0:T(8,128)(2,1)} fusion(bf16[2,512,384]{2,1,0:T(8,128)(2,1)} %get-tuple-element.255, s32[]{:T(128)S(6)} %copy.27, bf16[2048,384]{1,0:T(8,128)(2,1)} %get-tuple-element.264, s32[512]{0:T(512)S(1)} %bitcast.71, s32[512]{0:T(512)S(1)} %bitcast.72, s32[512]{0:T(512)S(1)} %bitcast.73, s32[512]{0:T(512)S(1)} %bitcast.74, ...), kind=kOutput, calls=%fused_computation.67.clone.1 | convolution fusion | flops 858128384 | bytes 1993732 | tf_op jit(solution)/shard_map/while/body/eval_jaxpr/dot_general | solution.py:22
  91.6 6.4 %gather_fusion.1 = bf16[1024,384]{1,0:T(8,128)(2,1)} fusion(bf16[2048,384]{1,0:T(8,128)(2,1)} %bitcast.4, s32[1024]{0:T(1024)S(1)} %fusion.113), kind=kCustom, calls=%fused_computation.1 | custom fusion | bytes 1576960 | tf_op jit(solution)/shard_map/gather | solution.py:50
  98.0 0.0 all-gather.3.cloned.1.call-done
  98.0 0.0 copy-start.1
  98.0 2.0 %fusion.109 = f32[1024,512]{1,0:T(8,128)S(1)} fusion(bf16[1024,384]{1,0:T(8,128)(2,1)} %gather_fusion.1, bf16[1536,512]{1,0:T(8,128)(2,1)} %all-gather.3.cloned.1.call-done, s32[]{:T(128)S(6)} %select_n.28), kind=kOutput, calls=%fused_computation.120 | convolution fusion | flops 402653184 | bytes 3276804 | tf_op jit(solution)/shard_map/dot_general | solution.py:55
  100.0 0.0 copy-done.1
  100.0 0.0 copy-start.8
  100.1 0.0 copy-start.9
  100.1 0.0 copy-start.3
  100.1 0.0 copy-start.7
  100.1 0.0 copy-start.6
  100.1 3.0 %convolution_add_fusion = f32[1024,512]{1,0:T(8,128)} fusion(f32[1024,512]{1,0:T(8,128)S(1)} %fusion.109, bf16[1024,384]{1,0:T(8,128)(2,1)S(1)} %bitcast.69, bf16[1536,512]{1,0:T(8,128)(2,1)} %all-gather.3.cloned.1.call-done, s32[]{:T(128)S(6)} %select_n.29), kind=kOutput, calls=%fused_computation.81 | convolution fusion | flops 403177472 | bytes 5373956 | tf_op jit(solution)/shard_map/dot_general | solution.py:56
  103.1 0.0 reduce-scatter.2.cloned.1.call-update
  103.2 0.0 copy-done.8
  103.2 0.1 dynamic_slice.28
  103.2 0.0 copy-done.9
  103.2 0.1 dynamic_slice.29
  103.3 0.0 copy-done.3
  103.3 0.0 copy-done.7
  103.4 0.0 copy-done.6
  103.4 11.2 %reduce-scatter.2.cloned.1.call-done = f32[1024,256]{1,0:T(8,128)} async-done(((f32[1024,512]{1,0:T(8,128)}), f32[1024,256]{1,0:T(8,128)}) %reduce-scatter.2.cloned.1.call-update) | async-done | bytes 1048592 | tf_op jit(solution)/shard_map/reduce_scatter | solution.py:58
  114.6 2.1 %maximum_convert_fusion = bf16[1024,256]{1,0:T(8,128)(2,1)} fusion(f32[1024,256]{1,0:T(8,128)} %reduce-scatter.2.cloned.1.call-done, f32[256]{0:T(256)S(1)} %dynamic_slice.28), kind=kLoop, calls=%fused_computation.91 | loop fusion | flops 786432 | bytes 1573888 | tf_op jit(solution)/shard_map/convert_element_type | solution.py:59
  116.7 2.1 %gather_fusion.2 = bf16[256,256]{1,0:T(8,128)(2,1)S(1)} fusion(bf16[1024,256]{1,0:T(8,128)(2,1)} %maximum_convert_fusion, s32[1024]{0:T(1024)S(1)} %pad_clamp_fusion), kind=kCustom, calls=%fused_computation.2 | custom fusion | bytes 263168 | tf_op jit(solution)/shard_map/gather | solution.py:62
  118.8 0.0 copy-start.10
  118.8 2.1 %all-gather = bf16[256,512]{1,0:T(8,128)(2,1)S(1)} all-gather(bf16[256,256]{1,0:T(8,128)(2,1)S(1)} %gather_fusion.2), channel_id=2, replica_groups=mesh['dom'=16,'mp'=2] {'mp'}, dimensions={1}, use_global_device_ids=true | all-gather | bytes 393216 | tf_op jit(solution)/shard_map/all_gather | solution.py:62
  121.0 2.5 %fusion.75 = bf16[256,256]{1,0:T(8,128)(2,1)S(1)} fusion(bf16[1024,256]{1,0:T(8,128)(2,1)} %maximum_convert_fusion, s32[256]{0:T(256)S(1)} %bitcast.86, s32[256]{0:T(256)S(1)} %bitcast.87, s32[256]{0:T(256)S(1)} %bitcast.84, s32[256]{0:T(256)S(1)} %bitcast.85, s32[256]{0:T(256)S(1)} %bitcast.83, pred[256]{0:T(512)(128)(4,1)S(1)} %get-tuple-element.170, ...), kind=kOutput, calls=%fused_computation.85 | convolution fusion | flops 140902400 | bytes 662784 | tf_op jit(solution)/shard_map/while/body/eval_jaxpr/dot_general | solution.py:22
  123.4 2.0 %all_gather.11 = bf16[256,512]{1,0:T(8,128)(2,1)S(1)} all-gather(bf16[256,256]{1,0:T(8,128)(2,1)S(1)} %fusion.75), channel_id=1, replica_groups=mesh['dom'=16,'mp'=2] {'mp'}, dimensions={1}, use_global_device_ids=true | all-gather | bytes 393216 | tf_op jit(solution)/shard_map/all_gather | solution.py:63
  125.4 0.0 copy-done.10
  125.4 0.4 multiply_reduce_fusion
  125.8 2.5 %psum.7 = f32[256]{0:T(256)S(1)} all-reduce(f32[256]{0:T(256)S(1)} %get-tuple-element.171), channel_id=1, replica_groups=mesh['dom'=16,'mp'=2] {'mp'}, use_global_device_ids=true, to_apply=%region_4.5 | all-reduce | flops 256 | bytes 2048 | tf_op jit(solution)/shard_map/psum | solution.py:66
  128.3 0.8 copy.18
  (20 shorter events, 0.2 us)
Async XLA Ops:
  6.5 15.8 %copy-start = (bf16[4096,384]{1,0:T(8,128)(2,1)S(1)}, bf16[4096,384]{1,0:T(8,128)(2,1)}, u32[]{:S(2)}) copy-start(bf16[4096,384]{1,0:T(8,128)(2,1)} %param.14) | copy-start | bytes 9437188
  31.4 5.3 %copy-start.4 = (s32[1024]{0:T(1024)S(1)}, s32[1024]{0:T(1024)}, u32[]{:S(2)}) copy-start(s32[1024]{0:T(1024)} %param.22) | copy-start | bytes 12292
  31.4 5.4 %copy-start.2 = (s32[1024,10]{0,1:T(8,128)S(1)}, s32[1024,10]{0,1:T(8,128)}, u32[]{:S(2)}) copy-start(s32[1024,10]{0,1:T(8,128)} %param.20) | copy-start | bytes 122884
  31.4 5.4 %copy-start.5 = (s32[1024]{0:T(1024)S(1)}, s32[1024]{0:T(1024)}, u32[]{:S(2)}) copy-start(s32[1024]{0:T(1024)} %param.21) | copy-start | bytes 12292
  31.4 37.8 %all-to-all-start.1 = ((bf16[16,128,384]{2,1,0:T(8,128)(2,1)}), bf16[16,128,384]{2,1,0:T(8,128)(2,1)}, u32[]{:S(2)}, u32[]{:S(2)}) async-start(bf16[16,128,384]{2,1,0:T(8,128)(2,1)} %bitcast.67), calls=%async_computation.1 | async-start | bytes 3145728 | tf_op jit(solution)/shard_map/all_to_all | solution.py:48
  36.0 62.1 %all-gather.3.cloned.1.call-start = ((), (), s32[]{:S(2)}) async-start(), calls=%async_computation.3 | async-start | bytes 2359296 | tf_op jit(solution)/shard_map/all_gather | solution.py:52
  36.7 77.9 %reduce-scatter.2.cloned.1.call-start = ((), (), s32[]{:S(2)}) async-start(), calls=%async_computation.4 | async-start | bytes 3145728 | tf_op jit(solution)/shard_map/reduce_scatter | solution.py:58
  98.0 2.0 %copy-start.1 = (bf16[2,512,384]{2,1,0:T(8,128)(2,1)S(1)}, bf16[2,512,384]{2,1,0:T(8,128)(2,1)}, u32[]{:S(2)}) copy-start(bf16[2,512,384]{2,1,0:T(8,128)(2,1)} %get-tuple-element.82) | copy-start | bytes 2359300
  100.0 3.1 %copy-start.8 = (f32[512]{0:T(512)S(1)}, f32[512]{0:T(512)}, u32[]{:S(2)}) copy-start(f32[512]{0:T(512)} %param.16) | copy-start | bytes 6148
  100.1 3.2 %copy-start.9 = (f32[512]{0:T(512)S(1)}, f32[512]{0:T(512)}, u32[]{:S(2)}) copy-start(f32[512]{0:T(512)} %param.18) | copy-start | bytes 6148
  100.1 3.3 %copy-start.3 = (s32[256]{0:T(256)S(1)}, s32[256]{0:T(256)}, u32[]{:S(2)}) copy-start(s32[256]{0:T(256)} %param.25) | copy-start | bytes 3076
  100.1 3.2 %copy-start.7 = (s32[256]{0:T(256)S(1)}, s32[256]{0:T(256)}, u32[]{:S(2)}) copy-start(s32[256]{0:T(256)} %param.24) | copy-start | bytes 3076
  100.1 3.3 %copy-start.6 = (s32[256,5]{0,1:T(8,128)S(1)}, s32[256,5]{0,1:T(8,128)}, u32[]{:S(2)}) copy-start(s32[256,5]{0,1:T(8,128)} %param.23) | copy-start | bytes 15364
  118.8 6.6 %copy-start.10 = (bf16[1024,256]{1,0:T(8,128)(2,1)S(1)}, bf16[1024,256]{1,0:T(8,128)(2,1)}, u32[]{:S(2)}) copy-start(bf16[1024,256]{1,0:T(8,128)(2,1)} %param.17) | copy-start | bytes 1572868
Sparse Core Ops, SparseCore 0:
  38.3 10.6 all-gather.2
  103.3 11.2 reduce-scatter.1
where the time goes:
time: 136 us
  waiting for transfers between devices  44.3 us (33%)
  matrix products  30 us (22%)
  blocking collectives  22.4 us (16%)
  local copies, waits for them, and re-layouts  18.7 us (14%)
  between operations  13.6 us (10%)
  starting transfers between devices  4.61 us (3%)
  other arithmetic  2.36 us (2%)
    all_to_all x1, waiting for transfers between devices, shards(): lax.all_to_all(found, 'dom', split_axis=0, concat_axis=0, tiled=True)  32.3 us
    dot_general x3, matrix products, one_block(): total = jnp.dot(weights, source, preferred_element_type=jnp.float32)  24.6 us
    all_to_all x1, blocking collectives, shards(): lax.all_to_all(asked, 'dom', split_axis=0, concat_axis=0, tiled=True)  15.8 us
    reduce_scatter x1, waiting for transfers between devices, shards(): lax.psum_scatter(partial_value, 'mp', scatter_dimension=1, tiled=True)  11.2 us
    gather x1, local copies, waits for them, and re-layouts, shards(): table[lax.all_to_all(asked, 'dom', split_axis=0, concat_axis=0, tiled=True)]  9.04 us
    gather x1, local copies, waits for them, and re-layouts, shards(): own_rows = fetched[self_a]  6.45 us
    all_to_all x1, starting transfers between devices, shards(): lax.all_to_all(found, 'dom', split_axis=0, concat_axis=0, tiled=True)  4.53 us
    dot_general x1, matrix products, shards(): jnp.dot(mean_a, near_weight, preferred_element_type=jnp.float32)  3.02 us
  transfers between devices with their start and end apart: 3, of which 2 were waited for; matrix products, arithmetic and copies ran while one was open for 21% of the time, Pallas kernels for 0%

commit v1 on v0

v1 whole, which is shorter than its diff:
```python
import functools

import jax
import jax.numpy as jnp
from jax import lax
from jax.experimental import pallas as pl
from jax.experimental.pallas import tpu as pltpu
from jax.sharding import PartitionSpec as P

MESH = pl.DeviceIdType.MESH
VMEM = pl.BlockSpec(memory_space=pltpu.VMEM)
TILE = 256


def peer(me, step, n):
    return lax.rem(me + 1 + lax.rem(n // 2 - 1 + step, n - 1), n)


def greet(me, n, partner):
    barrier = pltpu.get_barrier_semaphore()

    def one(step, carry):
        pl.semaphore_signal(
            barrier, inc=1, device_id={"dom": peer(me, step, n)}, device_id_type=MESH
        )
        return carry

    lax.fori_loop(0, n - 1, one, 0)
    if partner is not None:
        pl.semaphore_signal(barrier, inc=1, device_id={"mp": partner}, device_id_type=MESH)
    pl.semaphore_wait(barrier, n - 1 + (partner is not None))


def block_copy(source, landed, me, other, send_sem, recv_sem):
    return pltpu.make_async_remote_copy(
        src_ref=source.at[other],
        dst_ref=landed.at[me],
        send_sem=send_sem.at[other],
        recv_sem=recv_sem.at[me],
        device_id={"dom": other},
        device_id_type=MESH,
    )


def send_blocks(source, landed, me, n, send_sem, recv_sem):
    def one(step, carry):
        block_copy(source, landed, me, peer(me, step, n), send_sem, recv_sem).start()
        return carry

    lax.fori_loop(0, n - 1, one, 0)


def finish_sends(source, landed, me, n, send_sem, recv_sem):
    def one(step, carry):
        block_copy(source, landed, me, peer(me, step, n), send_sem, recv_sem).wait_send()
        return carry

    lax.fori_loop(0, n - 1, one, 0)


def wait_block(source, landed, other, recv_sem):
    pltpu.make_async_copy(source.at[other], landed.at[other], recv_sem.at[other]).wait()


def ask_kernel(n, asked_ref, out_ref, landed, send_sem, recv_sem):
    me = lax.axis_index("dom")
    greet(me, n, None)
    send_blocks(asked_ref, landed, me, n, send_sem, recv_sem)
    pltpu.make_async_copy(asked_ref.at[me], landed.at[me], recv_sem.at[me]).start()

    def one(other, carry):
        wait_block(asked_ref, landed, other, recv_sem)
        return carry

    lax.fori_loop(0, n, one, 0)
    out_ref[...] = landed[...]
    finish_sends(asked_ref, landed, me, n, send_sem, recv_sem)


def ask(asked, n):
    return pl.pallas_call(
        functools.partial(ask_kernel, n),
        out_shape=jax.ShapeDtypeStruct(asked.shape, asked.dtype),
        in_specs=[VMEM],
        out_specs=VMEM,
        scratch_shapes=[
            pltpu.VMEM(asked.shape, asked.dtype),
            pltpu.SemaphoreType.DMA((n,)),
            pltpu.SemaphoreType.DMA((n,)),
        ],
        compiler_params=pltpu.CompilerParams(collective_id=0, has_side_effects=True),
        name="ask",
    )(asked)


def build_picks(index_ref, fan, mean_pick, own_pick):
    rows, columns = mean_pick.shape
    high, wide = 64, min(512, columns)

    def one(at, carry):
        r0 = pl.multiple_of(at // (columns // wide) * high, high)
        c0 = pl.multiple_of(at % (columns // wide) * wide, wide)
        index = index_ref[pl.ds(r0, high), :]
        column = lax.broadcasted_iota(jnp.int32, (high, wide), 1) + c0
        total = jnp.zeros((high, wide), jnp.float32)
        for j in range(fan):
            total = total + jnp.where(index[:, j : j + 1] == column, 1.0, 0.0)
        mean_pick[pl.ds(r0, high), pl.ds(c0, wide)] = total.astype(jnp.bfloat16)
        own = jnp.where(index[:, fan : fan + 1] == column, 1.0, 0.0)
        own_pick[pl.ds(r0, high), pl.ds(c0, wide)] = own.astype(jnp.bfloat16)
        return carry

    lax.fori_loop(0, rows // high * (columns // wide), one, 0)


def dot(a, b):
    return jnp.dot(a, b, preferred_element_type=jnp.float32)


def main_kernel(
    n, fan_a, fan_b,
    found_ref, index_a_ref, index_b_ref, weight_a_ref, bias_a_ref, weight_b_ref, bias_b_ref,
    out_ref,
    fetched, pick_a, self_pick_a, pick_b, self_pick_b, sum_mean, sum_own,
    mine_a, theirs_a, hidden, mine_b, theirs_b, mine_sq, theirs_sq,
    send_sem, recv_sem, mp_send, mp_recv,
):
    me = lax.axis_index("dom")
    core = lax.axis_index("mp")
    partner = 1 - core
    each, half = found_ref.shape[1], found_ref.shape[2]
    rows = sum_mean.shape[0]
    half_hidden = hidden.shape[1]
    feature, hidden_width = weight_a_ref.shape[0] // 2, weight_b_ref.shape[0] // 2
    seeds = out_ref.shape[0]

    greet(me, n, partner)
    send_blocks(found_ref, fetched, me, n, send_sem, recv_sem)
    pltpu.make_async_copy(found_ref.at[me], fetched.at[me], recv_sem.at[me]).start()
    build_picks(index_a_ref, fan_a, pick_a, self_pick_a)
    build_picks(index_b_ref, fan_b, pick_b, self_pick_b)
    sum_mean[...] = jnp.zeros_like(sum_mean)
    sum_own[...] = jnp.zeros_like(sum_own)

    per = min(n, max(1, 256 // each))
    groups = n // per
    depth = per * each

    def one_group(step, carry):
        group = lax.rem(me // per + step, groups)

        def arrive(i, inner):
            wait_block(found_ref, fetched, group * per + i, recv_sem)
            return inner

        lax.fori_loop(0, per, arrive, 0)
        columns = pl.ds(pl.multiple_of(group * depth, depth), depth)

        def one_tile(tile, inner):
            at = pl.ds(pl.multiple_of(tile * TILE, TILE), TILE)
            block = fetched[pl.ds(group * per, per)].reshape(depth, half)
            sum_mean[at, :] += dot(pick_a[at, columns], block)
            sum_own[at, :] += dot(self_pick_a[at, columns], block)
            return inner

        lax.fori_loop(0, rows // TILE, one_tile, 0)
        return carry

    lax.fori_loop(0, groups, one_group, 0)

    def swap(source, landed, at):
        return pltpu.make_async_remote_copy(
            src_ref=source,
            dst_ref=landed,
            send_sem=mp_send.at[at],
            recv_sem=mp_recv.at[at],
            device_id={"mp": partner},
            device_id_type=MESH,
        )

    mine_a[0] = sum_own[...].astype(jnp.bfloat16)
    count_a = index_a_ref[:, fan_a + 1 : fan_a + 2].astype(jnp.float32)
    mine_a[1] = (sum_mean[...] / count_a).astype(jnp.bfloat16)
    swap_a = swap(mine_a, theirs_a, 0)
    swap_a.start()

    def rows_of(weight_ref, start, width, which):
        return weight_ref[pl.ds(pl.multiple_of(start + which * width, 128), width), :]

    def layer_a(tile, carry):
        at = pl.ds(pl.multiple_of(tile * TILE, TILE), TILE)
        value = dot(mine_a[0, at, :], rows_of(weight_a_ref, 0, half, core))
        value = value + dot(mine_a[1, at, :], rows_of(weight_a_ref, feature, half, core))
        sum_own[at, pl.ds(0, half_hidden)] = value
        return carry

    def layer_a_rest(tile, carry):
        at = pl.ds(pl.multiple_of(tile * TILE, TILE), TILE)
        value = sum_own[at, pl.ds(0, half_hidden)]
        value = value + dot(theirs_a[0, at, :], rows_of(weight_a_ref, 0, half, partner))
        value = value + dot(theirs_a[1, at, :], rows_of(weight_a_ref, feature, half, partner))
        hidden[at, :] = jnp.maximum(value + bias_a_ref[...], 0.0).astype(jnp.bfloat16)
        return carry

    lax.fori_loop(0, rows // TILE, layer_a, 0)
    swap_a.wait()
    lax.fori_loop(0, rows // TILE, layer_a_rest, 0)

    mine_b[0] = dot(self_pick_b[...], hidden[...]).astype(jnp.bfloat16)
    count_b = index_b_ref[:, fan_b + 1 : fan_b + 2].astype(jnp.float32)
    mine_b[1] = (dot(pick_b[...], hidden[...]) / count_b).astype(jnp.bfloat16)
    swap_b = swap(mine_b, theirs_b, 1)
    swap_b.start()
    state = dot(mine_b[0], rows_of(weight_b_ref, 0, half_hidden, core))
    state = state + dot(mine_b[1], rows_of(weight_b_ref, hidden_width, half_hidden, core))
    swap_b.wait()
    state = state + dot(theirs_b[0], rows_of(weight_b_ref, 0, half_hidden, partner))
    state = state + dot(theirs_b[1], rows_of(weight_b_ref, hidden_width, half_hidden, partner))
    state = jnp.maximum(state + bias_b_ref[...], 0.0)
    mine_sq[...] = jnp.broadcast_to(jnp.sum(state * state, axis=1, keepdims=True), mine_sq.shape)
    swap_sq = swap(mine_sq, theirs_sq, 2)
    swap_sq.start()
    swap_sq.wait()
    squares = mine_sq[:, 0:1] + theirs_sq[:, 0:1]
    scale = jnp.sqrt(jnp.float32(hidden_width)) / jnp.sqrt(squares + hidden_width)
    out_ref[...] = (state * scale).astype(out_ref.dtype)
    finish_sends(found_ref, fetched, me, n, send_sem, recv_sem)


def main(n, fan_a, fan_b, found, index_a, index_b, weight_a, bias_a, weight_b, bias_b):
    slots = found.shape[0] * found.shape[1]
    half, rows, seeds = found.shape[2], index_a.shape[0], index_b.shape[0]
    half_hidden = weight_a.shape[1]
    bf16, f32 = jnp.bfloat16, jnp.float32
    return pl.pallas_call(
        functools.partial(main_kernel, n, fan_a, fan_b),
        out_shape=jax.ShapeDtypeStruct((seeds, half_hidden), bf16),
        in_specs=[VMEM] * 7,
        out_specs=VMEM,
        scratch_shapes=[
            pltpu.VMEM(found.shape, bf16),
            pltpu.VMEM((rows, slots), bf16),
            pltpu.VMEM((rows, slots), bf16),
            pltpu.VMEM((seeds, rows), bf16),
            pltpu.VMEM((seeds, rows), bf16),
            pltpu.VMEM((rows, half), f32),
            pltpu.VMEM((rows, half), f32),
            pltpu.VMEM((2, rows, half), bf16),
            pltpu.VMEM((2, rows, half), bf16),
            pltpu.VMEM((rows, half_hidden), bf16),
            pltpu.VMEM((2, seeds, half_hidden), bf16),
            pltpu.VMEM((2, seeds, half_hidden), bf16),
            pltpu.VMEM((seeds, 128), f32),
            pltpu.VMEM((seeds, 128), f32),
            pltpu.SemaphoreType.DMA((n,)),
            pltpu.SemaphoreType.DMA((n,)),
            pltpu.SemaphoreType.DMA((3,)),
            pltpu.SemaphoreType.DMA((3,)),
        ],
        compiler_params=pltpu.CompilerParams(collective_id=1, has_side_effects=True),
        name="sage",
    )(found, index_a, index_b, weight_a, bias_a, weight_b, bias_b)


def with_counts(near, own, count):
    fan = near.shape[1]
    column = lax.broadcasted_iota(jnp.int32, (1, fan), 1)
    kept = jnp.where(column < count[:, None], near, -1)
    return jnp.concatenate([kept, own[:, None], count[:, None]], axis=1)


def shards(
    n,
    table,
    weight_a,
    bias_a,
    weight_b,
    bias_b,
    requests,
    near_a,
    self_a,
    count_a,
    near_b,
    self_b,
    count_b,
):
    half_hidden = weight_a.shape[1]
    core = lax.axis_index("mp")
    asked = ask(requests[0][:, None, :], n)[:, 0, :]
    found = table[asked]
    bias_a = lax.dynamic_slice_in_dim(bias_a, core * half_hidden, half_hidden, 0)[None, :]
    bias_b = lax.dynamic_slice_in_dim(bias_b, core * half_hidden, half_hidden, 0)[None, :]
    index_a = with_counts(near_a, self_a, count_a)
    index_b = with_counts(near_b, self_b, count_b)
    return main(
        n, near_a.shape[1], near_b.shape[1],
        found, index_a, index_b, weight_a, bias_a, weight_b, bias_b,
    )


def solution(mesh):
    placed = (
        P("dom", "mp"),
        P(None, "mp"),
        P(),
        P(None, "mp"),
        P(),
        P("dom", None, None),
        P("dom", None),
        P("dom"),
        P("dom"),
        P("dom", None),
        P("dom"),
        P("dom"),
    )
    return jax.shard_map(
        functools.partial(shards, mesh.shape["dom"]),
        mesh=mesh, in_specs=placed, out_specs=P("dom", "mp"), check_vma=False,
    )
```

time: 136 us -> 86.9 us (0.64)
  the two profiles are of different devices: /device:TPU:0 before, /device:TPU:15 now
where the time goes in v1:
time: 86.9 us; the launch traced here: 86.4 us
  Pallas kernels  67.4 us (78%)
  local copies, waits for them, and re-layouts  15.3 us (18%)
  other arithmetic  3.68 us (4%)
    pallas_call x1, Pallas kernels, main(): pl.pallas_call(functools.partial(main_kernel, n, fan_a, fan_b), out_shape...  59.2 us
    gather x1, local copies, waits for them, and re-layouts, shards(): found = table[asked]  9.07 us
    pallas_call x1, Pallas kernels, ask(): pl.pallas_call(functools.partial(ask_kernel, n), out_shape=jax.ShapeDtype...  8.19 us
    concatenate x2, local copies, waits for them, and re-layouts, with_counts(): return jnp.concatenate([kept, own[:, None], count[:, None]], axis=1)  1.84 us

profile of v1, /device:TPU:15, one launch (start us, length us, event | category | flops | bytes accessed | tf_op | source)
XLA Modules:
  0.0 86.4 jit_solution(6884461244050556679)
XLA Ops:
  0.0 0.0 copy-start
  0.0 1.5 %dynamic_slice.6 = f32[256]{0:T(256)} dynamic-slice(f32[512]{0:T(512)} %param.14, s32[]{:T(128)S(6)} %select_n.25), dynamic_slice_sizes={256} | dynamic-slice | bytes 2052 | tf_op jit(solution)/shard_map/dynamic_slice | solution.py:291
  1.5 1.3 %dynamic_slice.7 = f32[256]{0:T(256)} dynamic-slice(f32[512]{0:T(512)} %param.16, s32[]{:T(128)S(6)} %select_n.25), dynamic_slice_sizes={256} | dynamic-slice | bytes 2052 | tf_op jit(solution)/shard_map/dynamic_slice | solution.py:292
  2.8 8.2 %ask.1 = s32[16,1,128]{2,1,0:T(1,128)} custom-call(s32[16,1,128]{2,1,0:T(1,128)} %bitcast.16), custom_call_target="tpu_custom_call" | custom-call | tf_op jit(solution)/shard_map/ask/pallas_call | solution.py:81
  11.0 0.7 fusion.2
  11.7 0.7 fusion.3
  12.4 0.7 pad_add_fusion.1
  13.1 0.8 fusion
  14.0 0.7 pad_add_fusion
  14.7 0.8 copy.26.index_b_ref
  15.5 1.0 %copy.25.index_a_ref = s32[1024,12]{1,0:T(8,128)} copy(s32[1024,12]{0,1:T(8,128)S(1)} %pad_add_fusion) | data formatting | bytes 98304 | tf_op jit(solution)/shard_map/concatenate | solution.py:269
  16.5 0.0 copy-done
  16.5 9.1 %gather_fusion = bf16[2048,384]{1,0:T(8,128)(2,1)} fusion(bf16[4096,384]{1,0:T(8,128)(2,1)S(1)} %copy-done, s32[2048]{0:T(1024)S(1)} %fusion.2), kind=kCustom, calls=%fused_computation | custom fusion | bytes 3153920 | tf_op jit(solution)/shard_map/gather | solution.py:290
  25.6 59.2 %sage.1 = bf16[256,256]{1,0:T(8,128)(2,1)} custom-call(bf16[16,128,384]{2,1,0:T(8,128)(2,1)} %bitcast.13, s32[1024,12]{1,0:T(8,128)} %copy.25.index_a_ref, s32[256,7]{1,0:T(8,128)} %copy.26.index_b_ref, bf16[1536,256]{1,0:T(8,128)(2,1)} %weight_a_ref.1, f32[1,256]{1,0:T(1,128)} %bitcast.17, bf16[1024,256]{1,0:T(8,128)(2,1)} %weight_b_ref.1, f32[1,256]{1,0:T(1,128)} %bitcast.18), custom_call_target="tpu_custom_call" | custom-call | tf_op jit(solution)/shard_map/sage/pallas_call | solution.py:235
  84.9 1.6 %copy.28 = bf16[256,256]{1,0:T(8,128)(2,1)} copy(bf16[256,256]{1,0:T(8,128)(2,1)} %sage.1) | data formatting | bytes 262144
Async XLA Ops:
  0.0 16.5 %copy-start = (bf16[4096,384]{1,0:T(8,128)(2,1)S(1)}, bf16[4096,384]{1,0:T(8,128)(2,1)}, u32[]{:S(2)}) copy-start(bf16[4096,384]{1,0:T(8,128)(2,1)} %param.12) | copy-start | bytes 9437188

commit v2 on v1

--- a/solution.py
+++ b/solution.py
@@ -60,37 +60,6 @@
 
 def wait_block(source, landed, other, recv_sem):
     pltpu.make_async_copy(source.at[other], landed.at[other], recv_sem.at[other]).wait()
-
-
-def ask_kernel(n, asked_ref, out_ref, landed, send_sem, recv_sem):
-    me = lax.axis_index("dom")
-    greet(me, n, None)
-    send_blocks(asked_ref, landed, me, n, send_sem, recv_sem)
-    pltpu.make_async_copy(asked_ref.at[me], landed.at[me], recv_sem.at[me]).start()
-
-    def one(other, carry):
-        wait_block(asked_ref, landed, other, recv_sem)
-        return carry
-
-    lax.fori_loop(0, n, one, 0)
-    out_ref[...] = landed[...]
-    finish_sends(asked_ref, landed, me, n, send_sem, recv_sem)
-
-
-def ask(asked, n):
-    return pl.pallas_call(
-        functools.partial(ask_kernel, n),
-        out_shape=jax.ShapeDtypeStruct(asked.shape, asked.dtype),
-        in_specs=[VMEM],
-        out_specs=VMEM,
-        scratch_shapes=[
-            pltpu.VMEM(asked.shape, asked.dtype),
-            pltpu.SemaphoreType.DMA((n,)),
-            pltpu.SemaphoreType.DMA((n,)),
-        ],
-        compiler_params=pltpu.CompilerParams(collective_id=0, has_side_effects=True),
-        name="ask",
-    )(asked)
 
 
 def build_picks(index_ref, fan, mean_pick, own_pick):
@@ -117,13 +86,24 @@
     return jnp.dot(a, b, preferred_element_type=jnp.float32)
 
 
+def index_rows(index, near_ref, own_ref, count_ref):
+    fan, rows = near_ref.shape
+    count = count_ref[...]
+    pieces = [jnp.where(count > j, near_ref[j : j + 1, :], -1) for j in range(fan)]
+    pieces += [own_ref[...], count, jnp.zeros((index.shape[1] - fan - 2, rows), jnp.int32)]
+    index[...] = jnp.concatenate(pieces, axis=0).T
+
+
 def main_kernel(
-    n, fan_a, fan_b,
-    found_ref, index_a_ref, index_b_ref, weight_a_ref, bias_a_ref, weight_b_ref, bias_b_ref,
+    n,
+    asked_ref, table_ref, near_a_ref, self_a_ref, count_a_ref, near_b_ref, self_b_ref, count_b_ref,
+    weight_a_any, bias_a_ref, weight_b_any, bias_b_ref,
     out_ref,
+    table, table_wide, wanted, wanted_scalar, stage, found_ref,
+    weight_a_ref, weight_b_ref, index_a_ref, index_b_ref,
     fetched, pick_a, self_pick_a, pick_b, self_pick_b, sum_mean, sum_own,
     mine_a, theirs_a, hidden, mine_b, theirs_b, mine_sq, theirs_sq,
-    send_sem, recv_sem, mp_send, mp_recv,
+    ask_send, ask_recv, send_sem, recv_sem, mp_send, mp_recv, load_sem,
 ):
     me = lax.axis_index("dom")
     core = lax.axis_index("mp")
@@ -132,15 +112,64 @@
     rows = sum_mean.shape[0]
     half_hidden = hidden.shape[1]
     feature, hidden_width = weight_a_ref.shape[0] // 2, weight_b_ref.shape[0] // 2
-    seeds = out_ref.shape[0]
-
+    fan_a, fan_b = near_a_ref.shape[0], near_b_ref.shape[0]
+
+    load_table = pltpu.make_async_copy(table_ref, table, load_sem.at[0])
+    load_table.start()
     greet(me, n, partner)
-    send_blocks(found_ref, fetched, me, n, send_sem, recv_sem)
+    send_blocks(asked_ref, wanted, me, n, ask_send, ask_recv)
+    pltpu.make_async_copy(asked_ref.at[me], wanted.at[me], ask_recv.at[me]).start()
+    load_table.wait()
+    load_a = pltpu.make_async_copy(weight_a_any, weight_a_ref, load_sem.at[1])
+    load_a.start()
+    load_b = pltpu.make_async_copy(weight_b_any, weight_b_ref, load_sem.at[2])
+    load_b.start()
+
+    def widen(tile, carry):
+        at = pl.ds(pl.multiple_of(tile * 128, 128), 128)
+        table_wide[at, :] = table[at, :].astype(jnp.float32)
+        return carry
+
+    lax.fori_loop(0, table.shape[0] // 128, widen, 0)
+
+    def asked_of(other, carry):
+        wait_block(asked_ref, wanted, other, ask_recv)
+        return carry
+
+    lax.fori_loop(0, n, asked_of, 0)
+    to_scalar = pltpu.make_async_copy(wanted, wanted_scalar, load_sem.at[3])
+    to_scalar.start()
+    to_scalar.wait()
+
+    def find(other):
+        def some(at, carry):
+            r0 = at * 16
+            for k in range(16):
+                row = wanted_scalar[other, 0, r0 + k]
+                stage[pl.ds(r0 + k, 1), :] = table_wide[pl.ds(row, 1), :]
+            return carry
+
+        lax.fori_loop(0, each // 16, some, 0)
+        found_ref[other] = stage[...].astype(jnp.bfloat16)
+
+    def find_and_send(step, carry):
+        other = peer(me, step, n)
+        find(other)
+        block_copy(found_ref, fetched, me, other, send_sem, recv_sem).start()
+        return carry
+
+    lax.fori_loop(0, n - 1, find_and_send, 0)
+    find(me)
     pltpu.make_async_copy(found_ref.at[me], fetched.at[me], recv_sem.at[me]).start()
+    index_rows(index_a_ref, near_a_ref, self_a_ref, count_a_ref)
+    index_rows(index_b_ref, near_b_ref, self_b_ref, count_b_ref)
     build_picks(index_a_ref, fan_a, pick_a, self_pick_a)
     build_picks(index_b_ref, fan_b, pick_b, self_pick_b)
     sum_mean[...] = jnp.zeros_like(sum_mean)
     sum_own[...] = jnp.zeros_like(sum_own)
+    mine_cols = pl.ds(pl.multiple_of(core * half_hidden, 128), half_hidden)
+    load_a.wait()
+    load_b.wait()
 
     per = min(n, max(1, 256 // each))
     groups = n // per
@@ -199,7 +228,7 @@
         value = sum_own[at, pl.ds(0, half_hidden)]
         value = value + dot(theirs_a[0, at, :], rows_of(weight_a_ref, 0, half, partner))
         value = value + dot(theirs_a[1, at, :], rows_of(weight_a_ref, feature, half, partner))
-        hidden[at, :] = jnp.maximum(value + bias_a_ref[...], 0.0).astype(jnp.bfloat16)
+        hidden[at, :] = jnp.maximum(value + bias_a_ref[:, mine_cols], 0.0).astype(jnp.bfloat16)
         return carry
 
     lax.fori_loop(0, rows // TILE, layer_a, 0)
@@ -216,7 +245,7 @@
     swap_b.wait()
     state = state + dot(theirs_b[0], rows_of(weight_b_ref, 0, half_hidden, partner))
     state = state + dot(theirs_b[1], rows_of(weight_b_ref, hidden_width, half_hidden, partner))
-    state = jnp.maximum(state + bias_b_ref[...], 0.0)
+    state = jnp.maximum(state + bias_b_ref[:, mine_cols], 0.0)
     mine_sq[...] = jnp.broadcast_to(jnp.sum(state * state, axis=1, keepdims=True), mine_sq.shape)
     swap_sq = swap(mine_sq, theirs_sq, 2)
     swap_sq.start()
@@ -224,21 +253,48 @@
     squares = mine_sq[:, 0:1] + theirs_sq[:, 0:1]
     scale = jnp.sqrt(jnp.float32(hidden_width)) / jnp.sqrt(squares + hidden_width)
     out_ref[...] = (state * scale).astype(out_ref.dtype)
+    finish_sends(asked_ref, wanted, me, n, ask_send, ask_recv)
     finish_sends(found_ref, fetched, me, n, send_sem, recv_sem)
 
 
-def main(n, fan_a, fan_b, found, index_a, index_b, weight_a, bias_a, weight_b, bias_b):
-    slots = found.shape[0] * found.shape[1]
-    half, rows, seeds = found.shape[2], index_a.shape[0], index_b.shape[0]
-    half_hidden = weight_a.shape[1]
+def shards(
+    n,
+    table,
+    weight_a,
+    bias_a,
+    weight_b,
+    bias_b,
+    requests,
+    near_a,
+    self_a,
+    count_a,
+    near_b,
+    self_b,
+    count_b,
+):
+    each = requests.shape[2]
+    half, half_hidden = table.shape[1], weight_a.shape[1]
+    rows, seeds, slots = near_a.shape[0], near_b.shape[0], n * each
+    wide = -(-(near_a.shape[1] + 2) // 8) * 8
     bf16, f32 = jnp.bfloat16, jnp.float32
+    anywhere = pl.BlockSpec(memory_space=pl.ANY)
     return pl.pallas_call(
-        functools.partial(main_kernel, n, fan_a, fan_b),
+        functools.partial(main_kernel, n),
         out_shape=jax.ShapeDtypeStruct((seeds, half_hidden), bf16),
-        in_specs=[VMEM] * 7,
+        in_specs=[VMEM, anywhere] + [VMEM] * 6 + [anywhere, VMEM, anywhere, VMEM],
         out_specs=VMEM,
         scratch_shapes=[
-            pltpu.VMEM(found.shape, bf16),
+            pltpu.VMEM(table.shape, bf16),
+            pltpu.VMEM(table.shape, f32),
+            pltpu.VMEM((n, 1, each), jnp.int32),
+            pltpu.SMEM((n, 1, each), jnp.int32),
+            pltpu.VMEM((each, half), f32),
+            pltpu.VMEM((n, each, half), bf16),
+            pltpu.VMEM(weight_a.shape, bf16),
+            pltpu.VMEM(weight_b.shape, bf16),
+            pltpu.VMEM((rows, wide), jnp.int32),
+            pltpu.VMEM((seeds, wide), jnp.int32),
+            pltpu.VMEM((n, each, half), bf16),
             pltpu.VMEM((rows, slots), bf16),
             pltpu.VMEM((rows, slots), bf16),
             pltpu.VMEM((seeds, rows), bf16),
@@ -254,47 +310,20 @@
             pltpu.VMEM((seeds, 128), f32),
             pltpu.SemaphoreType.DMA((n,)),
             pltpu.SemaphoreType.DMA((n,)),
+            pltpu.SemaphoreType.DMA((n,)),
+            pltpu.SemaphoreType.DMA((n,)),
             pltpu.SemaphoreType.DMA((3,)),
             pltpu.SemaphoreType.DMA((3,)),
+            pltpu.SemaphoreType.DMA((4,)),
         ],
-        compiler_params=pltpu.CompilerParams(collective_id=1, has_side_effects=True),
+        compiler_params=pltpu.CompilerParams(
+            collective_id=0, has_side_effects=True, vmem_limit_bytes=60 * 1024 * 1024
+        ),
         name="sage",
-    )(found, index_a, index_b, weight_a, bias_a, weight_b, bias_b)
-
-
-def with_counts(near, own, count):
-    fan = near.shape[1]
-    column = lax.broadcasted_iota(jnp.int32, (1, fan), 1)
-    kept = jnp.where(column < count[:, None], near, -1)
-    return jnp.concatenate([kept, own[:, None], count[:, None]], axis=1)
-
-
-def shards(
-    n,
-    table,
-    weight_a,
-    bias_a,
-    weight_b,
-    bias_b,
-    requests,
-    near_a,
-    self_a,
-    count_a,
-    near_b,
-    self_b,
-    count_b,
-):
-    half_hidden = weight_a.shape[1]
-    core = lax.axis_index("mp")
-    asked = ask(requests[0][:, None, :], n)[:, 0, :]
-    found = table[asked]
-    bias_a = lax.dynamic_slice_in_dim(bias_a, core * half_hidden, half_hidden, 0)[None, :]
-    bias_b = lax.dynamic_slice_in_dim(bias_b, core * half_hidden, half_hidden, 0)[None, :]
-    index_a = with_counts(near_a, self_a, count_a)
-    index_b = with_counts(near_b, self_b, count_b)
-    return main(
-        n, near_a.shape[1], near_b.shape[1],
-        found, index_a, index_b, weight_a, bias_a, weight_b, bias_b,
+    )(
+        requests[0][:, None, :], table,
+        near_a.T, self_a[None, :], count_a[None, :], near_b.T, self_b[None, :], count_b[None, :],
+        weight_a, bias_a[None, :], weight_b, bias_b[None, :],
     )
 
 

time: 86.9 us -> 64.8 us (0.75)
  the two profiles are of different devices: /device:TPU:15 before, /device:TPU:0 now
where the time goes in v2:
time: 64.8 us; the launch traced here: 64 us
  Pallas kernels  62.4 us (96%)
  local copies, waits for them, and re-layouts  1.57 us (2%)
    pallas_call x1, Pallas kernels, shards(): pl.pallas_call(functools.partial(main_kernel, n), out_shape=jax.ShapeDtyp...  62.4 us
    unnamed x1, local copies, waits for them, and re-layouts  1.57 us

profile of v2, /device:TPU:0, one launch (start us, length us, event | category | flops | bytes accessed | tf_op | source)
XLA Modules:
  0.0 64.0 jit_solution(1676692951327177940)
XLA Ops:
  0.0 62.4 %sage.1 = bf16[256,256]{1,0:T(8,128)(2,1)} custom-call(s32[16,1,128]{2,1,0:T(1,128)} %bitcast.10, bf16[4096,384]{1,0:T(8,128)(2,1)} %table_ref.1, s32[10,1024]{1,0:T(8,128)} %bitcast.9, s32[1,1024]{1,0:T(1,128)} %bitcast.12, s32[1,1024]{1,0:T(1,128)} %bitcast.13, s32[5,256]{1,0:T(8,128)} %bitcast.11, s32[1,256]{1,0:T(1,128)} %bitcast.16, s32[1,256]{1,0:T(1,128)} %bitcast.17, ...), custom_call_target="tpu_custom_call" | custom-call | tf_op jit(solution)/shard_map/sage/pallas_call | solution.py:281
  62.4 1.6 %copy.14 = bf16[256,256]{1,0:T(8,128)(2,1)} copy(bf16[256,256]{1,0:T(8,128)(2,1)} %sage.1) | data formatting | bytes 262144

commit v3 on v2

--- a/solution.py
+++ b/solution.py
@@ -13,7 +13,13 @@
 
 
 def peer(me, step, n):
-    return lax.rem(me + 1 + lax.rem(n // 2 - 1 + step, n - 1), n)
+    if n & (n - 1):
+        return lax.rem(me + 1 + lax.rem(n // 2 - 1 + step, n - 1), n)
+    other, mask, bit = 0, n - 1 - step, 1
+    while bit < n:
+        other = other + lax.rem(me // bit + mask // bit, 2) * bit
+        bit *= 2
+    return other
 
 
 def greet(me, n, partner):
@@ -64,22 +70,30 @@
 
 def build_picks(index_ref, fan, mean_pick, own_pick):
     rows, columns = mean_pick.shape
-    high, wide = 64, min(512, columns)
+    high = 16
+    short = jnp.int16 if columns < 2**15 else jnp.int32
 
     def one(at, carry):
-        r0 = pl.multiple_of(at // (columns // wide) * high, high)
-        c0 = pl.multiple_of(at % (columns // wide) * wide, wide)
+        r0 = pl.multiple_of(at * high, high)
         index = index_ref[pl.ds(r0, high), :]
-        column = lax.broadcasted_iota(jnp.int32, (high, wide), 1) + c0
-        total = jnp.zeros((high, wide), jnp.float32)
-        for j in range(fan):
-            total = total + jnp.where(index[:, j : j + 1] == column, 1.0, 0.0)
-        mean_pick[pl.ds(r0, high), pl.ds(c0, wide)] = total.astype(jnp.bfloat16)
-        own = jnp.where(index[:, fan : fan + 1] == column, 1.0, 0.0)
-        own_pick[pl.ds(r0, high), pl.ds(c0, wide)] = own.astype(jnp.bfloat16)
-        return carry
-
-    lax.fori_loop(0, rows // high * (columns // wide), one, 0)
+        lanes = [
+            jnp.broadcast_to(index[:, j : j + 1], (high, 128)).astype(short)
+            for j in range(fan + 1)
+        ]
+        lane = lax.broadcasted_iota(jnp.int32, (high, 128), 1)
+        one_value, no_value = jnp.bfloat16(1.0), jnp.bfloat16(0.0)
+        for c in range(0, columns, 128):
+            column = (lane + c).astype(short)
+            total = jnp.where(lanes[0] == column, one_value, no_value)
+            for j in range(1, fan):
+                total = total + jnp.where(lanes[j] == column, one_value, no_value)
+            mean_pick[pl.ds(r0, high), c : c + 128] = total
+            own_pick[pl.ds(r0, high), c : c + 128] = jnp.where(
+                lanes[fan] == column, one_value, no_value
+            )
+        return carry
+
+    lax.fori_loop(0, rows // high, one, 0)
 
 
 def dot(a, b):
@@ -103,7 +117,7 @@
     weight_a_ref, weight_b_ref, index_a_ref, index_b_ref,
     fetched, pick_a, self_pick_a, pick_b, self_pick_b, sum_mean, sum_own,
     mine_a, theirs_a, hidden, mine_b, theirs_b, mine_sq, theirs_sq,
-    ask_send, ask_recv, send_sem, recv_sem, mp_send, mp_recv, load_sem,
+    ask_send, ask_recv, send_sem, recv_sem, mp_send, mp_recv, load_sem, scalar_sem,
 ):
     me = lax.axis_index("dom")
     core = lax.axis_index("mp")
@@ -131,17 +145,25 @@
         return carry
 
     lax.fori_loop(0, table.shape[0] // 128, widen, 0)
-
-    def asked_of(other, carry):
+    index_rows(index_a_ref, near_a_ref, self_a_ref, count_a_ref)
+    index_rows(index_b_ref, near_b_ref, self_b_ref, count_b_ref)
+
+    def to_scalar(other):
+        return pltpu.make_async_copy(wanted.at[other], wanted_scalar.at[other], scalar_sem.at[other])
+
+    def asked_of(step, carry):
+        other = peer(me, step, n)
         wait_block(asked_ref, wanted, other, ask_recv)
-        return carry
-
-    lax.fori_loop(0, n, asked_of, 0)
-    to_scalar = pltpu.make_async_copy(wanted, wanted_scalar, load_sem.at[3])
-    to_scalar.start()
-    to_scalar.wait()
+        to_scalar(other).start()
+        return carry
+
+    lax.fori_loop(0, n - 1, asked_of, 0)
+    wait_block(asked_ref, wanted, me, ask_recv)
+    to_scalar(me).start()
 
     def find(other):
+        to_scalar(other).wait()
+
         def some(at, carry):
             r0 = at * 16
             for k in range(16):
@@ -161,8 +183,6 @@
     lax.fori_loop(0, n - 1, find_and_send, 0)
     find(me)
     pltpu.make_async_copy(found_ref.at[me], fetched.at[me], recv_sem.at[me]).start()
-    index_rows(index_a_ref, near_a_ref, self_a_ref, count_a_ref)
-    index_rows(index_b_ref, near_b_ref, self_b_ref, count_b_ref)
     build_picks(index_a_ref, fan_a, pick_a, self_pick_a)
     build_picks(index_b_ref, fan_b, pick_b, self_pick_b)
     sum_mean[...] = jnp.zeros_like(sum_mean)
@@ -207,38 +227,39 @@
             device_id_type=MESH,
         )
 
-    mine_a[0] = sum_own[...].astype(jnp.bfloat16)
-    count_a = index_a_ref[:, fan_a + 1 : fan_a + 2].astype(jnp.float32)
-    mine_a[1] = (sum_mean[...] / count_a).astype(jnp.bfloat16)
-    swap_a = swap(mine_a, theirs_a, 0)
-    swap_a.start()
-
     def rows_of(weight_ref, start, width, which):
         return weight_ref[pl.ds(pl.multiple_of(start + which * width, 128), width), :]
 
+    def swap_a(tile):
+        return swap(mine_a.at[tile], theirs_a.at[tile], 2 + tile)
+
     def layer_a(tile, carry):
         at = pl.ds(pl.multiple_of(tile * TILE, TILE), TILE)
-        value = dot(mine_a[0, at, :], rows_of(weight_a_ref, 0, half, core))
-        value = value + dot(mine_a[1, at, :], rows_of(weight_a_ref, feature, half, core))
+        count = index_a_ref[at, fan_a + 1 : fan_a + 2].astype(jnp.float32)
+        mine_a[tile, 0] = sum_own[at, :].astype(jnp.bfloat16)
+        mine_a[tile, 1] = (sum_mean[at, :] / count).astype(jnp.bfloat16)
+        swap_a(tile).start()
+        value = dot(mine_a[tile, 0], rows_of(weight_a_ref, 0, half, core))
+        value = value + dot(mine_a[tile, 1], rows_of(weight_a_ref, feature, half, core))
         sum_own[at, pl.ds(0, half_hidden)] = value
         return carry
 
     def layer_a_rest(tile, carry):
         at = pl.ds(pl.multiple_of(tile * TILE, TILE), TILE)
+        swap_a(tile).wait()
         value = sum_own[at, pl.ds(0, half_hidden)]
-        value = value + dot(theirs_a[0, at, :], rows_of(weight_a_ref, 0, half, partner))
-        value = value + dot(theirs_a[1, at, :], rows_of(weight_a_ref, feature, half, partner))
+        value = value + dot(theirs_a[tile, 0], rows_of(weight_a_ref, 0, half, partner))
+        value = value + dot(theirs_a[tile, 1], rows_of(weight_a_ref, feature, half, partner))
         hidden[at, :] = jnp.maximum(value + bias_a_ref[:, mine_cols], 0.0).astype(jnp.bfloat16)
         return carry
 
     lax.fori_loop(0, rows // TILE, layer_a, 0)
-    swap_a.wait()
     lax.fori_loop(0, rows // TILE, layer_a_rest, 0)
 
     mine_b[0] = dot(self_pick_b[...], hidden[...]).astype(jnp.bfloat16)
     count_b = index_b_ref[:, fan_b + 1 : fan_b + 2].astype(jnp.float32)
     mine_b[1] = (dot(pick_b[...], hidden[...]) / count_b).astype(jnp.bfloat16)
-    swap_b = swap(mine_b, theirs_b, 1)
+    swap_b = swap(mine_b, theirs_b, 0)
     swap_b.start()
     state = dot(mine_b[0], rows_of(weight_b_ref, 0, half_hidden, core))
     state = state + dot(mine_b[1], rows_of(weight_b_ref, hidden_width, half_hidden, core))
@@ -247,7 +268,7 @@
     state = state + dot(theirs_b[1], rows_of(weight_b_ref, hidden_width, half_hidden, partner))
     state = jnp.maximum(state + bias_b_ref[:, mine_cols], 0.0)
     mine_sq[...] = jnp.broadcast_to(jnp.sum(state * state, axis=1, keepdims=True), mine_sq.shape)
-    swap_sq = swap(mine_sq, theirs_sq, 2)
+    swap_sq = swap(mine_sq, theirs_sq, 1)
     swap_sq.start()
     swap_sq.wait()
     squares = mine_sq[:, 0:1] + theirs_sq[:, 0:1]
@@ -301,8 +322,8 @@
             pltpu.VMEM((seeds, rows), bf16),
             pltpu.VMEM((rows, half), f32),
             pltpu.VMEM((rows, half), f32),
-            pltpu.VMEM((2, rows, half), bf16),
-            pltpu.VMEM((2, rows, half), bf16),
+            pltpu.VMEM((rows // TILE, 2, TILE, half), bf16),
+            pltpu.VMEM((rows // TILE, 2, TILE, half), bf16),
             pltpu.VMEM((rows, half_hidden), bf16),
             pltpu.VMEM((2, seeds, half_hidden), bf16),
             pltpu.VMEM((2, seeds, half_hidden), bf16),
@@ -312,9 +333,10 @@
             pltpu.SemaphoreType.DMA((n,)),
             pltpu.SemaphoreType.DMA((n,)),
             pltpu.SemaphoreType.DMA((n,)),
+            pltpu.SemaphoreType.DMA((2 + rows // TILE,)),
+            pltpu.SemaphoreType.DMA((2 + rows // TILE,)),
             pltpu.SemaphoreType.DMA((3,)),
-            pltpu.SemaphoreType.DMA((3,)),
-            pltpu.SemaphoreType.DMA((4,)),
+            pltpu.SemaphoreType.DMA((n,)),
         ],
         compiler_params=pltpu.CompilerParams(
             collective_id=0, has_side_effects=True, vmem_limit_bytes=60 * 1024 * 1024

time: 64.8 us -> 62.1 us (0.958); the launches traced: 64 us -> 61.9 us
  Pallas kernels: 62.4 us -> 60.3 us
    pallas_call x1, Pallas kernels: 62.4 us -> 60.3 us  [shards(): pl.pallas_call(functools.partial(main_kernel, n), out_shape=jax.ShapeDtyp...]
where the time goes in v3:
time: 62.1 us; the launch traced here: 61.9 us
  Pallas kernels  60.3 us (97%)
  local copies, waits for them, and re-layouts  1.57 us (3%)
    pallas_call x1, Pallas kernels, shards(): pl.pallas_call(functools.partial(main_kernel, n), out_shape=jax.ShapeDtyp...  60.3 us
    unnamed x1, local copies, waits for them, and re-layouts  1.57 us

profile of v3, /device:TPU:0, one launch (start us, length us, event | category | flops | bytes accessed | tf_op | source)
XLA Modules:
  0.0 61.9 jit_solution(1439112813298775808)
XLA Ops:
  0.0 60.3 %sage.1 = bf16[256,256]{1,0:T(8,128)(2,1)} custom-call(s32[16,1,128]{2,1,0:T(1,128)} %bitcast.10, bf16[4096,384]{1,0:T(8,128)(2,1)} %table_ref.1, s32[10,1024]{1,0:T(8,128)} %bitcast.9, s32[1,1024]{1,0:T(1,128)} %bitcast.12, s32[1,1024]{1,0:T(1,128)} %bitcast.13, s32[5,256]{1,0:T(8,128)} %bitcast.11, s32[1,256]{1,0:T(1,128)} %bitcast.16, s32[1,256]{1,0:T(1,128)} %bitcast.17, ...), custom_call_target="tpu_custom_call" | custom-call | tf_op jit(solution)/shard_map/sage/pallas_call | solution.py:302
  60.3 1.6 %copy.14 = bf16[256,256]{1,0:T(8,128)(2,1)} copy(bf16[256,256]{1,0:T(8,128)(2,1)} %sage.1) | data formatting | bytes 262144

commit v4 on v3

--- a/solution.py
+++ b/solution.py
@@ -15,7 +15,11 @@
 def peer(me, step, n):
     if n & (n - 1):
         return lax.rem(me + 1 + lax.rem(n // 2 - 1 + step, n - 1), n)
-    other, mask, bit = 0, n - 1 - step, 1
+    return exchanged(me, n - 1 - step, n)
+
+
+def exchanged(me, mask, n):
+    other, bit = 0, 1
     while bit < n:
         other = other + lax.rem(me // bit + mask // bit, 2) * bit
         bit *= 2
@@ -151,16 +155,6 @@
     def to_scalar(other):
         return pltpu.make_async_copy(wanted.at[other], wanted_scalar.at[other], scalar_sem.at[other])
 
-    def asked_of(step, carry):
-        other = peer(me, step, n)
-        wait_block(asked_ref, wanted, other, ask_recv)
-        to_scalar(other).start()
-        return carry
-
-    lax.fori_loop(0, n - 1, asked_of, 0)
-    wait_block(asked_ref, wanted, me, ask_recv)
-    to_scalar(me).start()
-
     def find(other):
         to_scalar(other).wait()
 
@@ -174,13 +168,29 @@
         lax.fori_loop(0, each // 16, some, 0)
         found_ref[other] = stage[...].astype(jnp.bfloat16)
 
+    behind = min(2, n - 1)
+
+    def asked_of(step):
+        other = peer(me, step, n)
+        wait_block(asked_ref, wanted, other, ask_recv)
+        to_scalar(other).start()
+
     def find_and_send(step, carry):
-        other = peer(me, step, n)
-        find(other)
-        block_copy(found_ref, fetched, me, other, send_sem, recv_sem).start()
-        return carry
-
-    lax.fori_loop(0, n - 1, find_and_send, 0)
+        @pl.when(step < n - 1)
+        def _():
+            asked_of(step)
+
+        @pl.when(step >= behind)
+        def _():
+            other = peer(me, step - behind, n)
+            find(other)
+            block_copy(found_ref, fetched, me, other, send_sem, recv_sem).start()
+
+        return carry
+
+    lax.fori_loop(0, n - 1 + behind, find_and_send, 0)
+    wait_block(asked_ref, wanted, me, ask_recv)
+    to_scalar(me).start()
     find(me)
     pltpu.make_async_copy(found_ref.at[me], fetched.at[me], recv_sem.at[me]).start()
     build_picks(index_a_ref, fan_a, pick_a, self_pick_a)
@@ -196,7 +206,7 @@
     depth = per * each
 
     def one_group(step, carry):
-        group = lax.rem(me // per + step, groups)
+        group = exchanged(me // per, lax.rem(groups - step, groups), groups)
 
         def arrive(i, inner):
             wait_block(found_ref, fetched, group * per + i, recv_sem)

time: 62.1 us -> 61.7 us (level)
  no operation moved by 1% of the time
where the time goes in v4:
time: 61.7 us; the launch traced here: 61.5 us
  Pallas kernels  59.9 us (97%)
  local copies, waits for them, and re-layouts  1.57 us (3%)
    pallas_call x1, Pallas kernels, shards(): pl.pallas_call(functools.partial(main_kernel, n), out_shape=jax.ShapeDtyp...  59.9 us
    unnamed x1, local copies, waits for them, and re-layouts  1.57 us

profile of v4, /device:TPU:0, one launch (start us, length us, event | category | flops | bytes accessed | tf_op | source)
XLA Modules:
  0.0 61.5 jit_solution(17760465620839810160)
XLA Ops:
  0.0 59.9 %sage.1 = bf16[256,256]{1,0:T(8,128)(2,1)} custom-call(s32[16,1,128]{2,1,0:T(1,128)} %bitcast.10, bf16[4096,384]{1,0:T(8,128)(2,1)} %table_ref.1, s32[10,1024]{1,0:T(8,128)} %bitcast.9, s32[1,1024]{1,0:T(1,128)} %bitcast.12, s32[1,1024]{1,0:T(1,128)} %bitcast.13, s32[5,256]{1,0:T(8,128)} %bitcast.11, s32[1,256]{1,0:T(1,128)} %bitcast.16, s32[1,256]{1,0:T(1,128)} %bitcast.17, ...), custom_call_target="tpu_custom_call" | custom-call | tf_op jit(solution)/shard_map/sage/pallas_call | solution.py:312
  59.9 1.6 %copy.14 = bf16[256,256]{1,0:T(8,128)(2,1)} copy(bf16[256,256]{1,0:T(8,128)(2,1)} %sage.1) | data formatting | bytes 262144

commit v5 on v4

--- a/solution.py
+++ b/solution.py
@@ -15,7 +15,7 @@
 def peer(me, step, n):
     if n & (n - 1):
         return lax.rem(me + 1 + lax.rem(n // 2 - 1 + step, n - 1), n)
-    return exchanged(me, n - 1 - step, n)
+    return exchanged(me, n - 1 - step // 2 - lax.rem(step, 2) * (n // 2), n)
 
 
 def exchanged(me, mask, n):

time: 61.7 us -> 62.3 us (level)
  Pallas kernels: 59.9 us -> 60.6 us
    pallas_call x1, Pallas kernels: 59.9 us -> 60.6 us  [shards(): pl.pallas_call(functools.partial(main_kernel, n), out_shape=jax.ShapeDtyp...]
where the time goes in v5:
time: 62.3 us; the launch traced here: 62.1 us
  Pallas kernels  60.6 us (97%)
  local copies, waits for them, and re-layouts  1.57 us (3%)
    pallas_call x1, Pallas kernels, shards(): pl.pallas_call(functools.partial(main_kernel, n), out_shape=jax.ShapeDtyp...  60.6 us
    unnamed x1, local copies, waits for them, and re-layouts  1.57 us

profile of v5, /device:TPU:0, one launch (start us, length us, event | category | flops | bytes accessed | tf_op | source)
XLA Modules:
  0.0 62.1 jit_solution(17566257199675191373)
XLA Ops:
  0.0 60.6 %sage.1 = bf16[256,256]{1,0:T(8,128)(2,1)} custom-call(s32[16,1,128]{2,1,0:T(1,128)} %bitcast.10, bf16[4096,384]{1,0:T(8,128)(2,1)} %table_ref.1, s32[10,1024]{1,0:T(8,128)} %bitcast.9, s32[1,1024]{1,0:T(1,128)} %bitcast.12, s32[1,1024]{1,0:T(1,128)} %bitcast.13, s32[5,256]{1,0:T(8,128)} %bitcast.11, s32[1,256]{1,0:T(1,128)} %bitcast.16, s32[1,256]{1,0:T(1,128)} %bitcast.17, ...), custom_call_target="tpu_custom_call" | custom-call | tf_op jit(solution)/shard_map/sage/pallas_call | solution.py:312
  60.6 1.6 %copy.14 = bf16[256,256]{1,0:T(8,128)(2,1)} copy(bf16[256,256]{1,0:T(8,128)(2,1)} %sage.1) | data formatting | bytes 262144
